TPU v7x, 32 devices: a whole 2x2x4 slice. The times are simulated.
32 devices in a mesh: gx: 2 (over x), gy: 4 (over y, core), gz: 4 (over z).
Axes of the slice: x: 2, y: 2, z: 4, core: 2. Of those that a mesh axis runs over, the one named last changes fastest.
Arguments:
- rhs: float32 [8, 8, 2, 16, 512], P(None, None, 'gx', 'gy', 'gz'), as said below
- blocks: bfloat16 [7, 8, 8, 2, 16, 512], P(None, None, None, 'gx', 'gy', 'gz'), as said below
Outputs:
- basis: float32 [4, 8, 8, 2, 16, 512], P(None, None, None, 'gx', 'gy', 'gz')
- hess: float32 [4, 8, 3, 8], replicated
Inputs may be any that keep to these rules, and one draw needn't show every extreme that they name: `rhs`: each cell's value is a random draw times a positive scale that varies smoothly over the grid. The operator couples each cell only to itself and its six face neighbours; its blocks are full and the block Krylov spaces keep full rank.
All inputs are finite; a program needn't handle non-finite values.
Results may differ from a plain program's by a relative error of at most 0.001.
Values sent between devices are 32-bit elements; how exact they have to be, the bound alone decides.
A program may use at most 64 MiB of HBM per device.

v0:
```python
import jax
import jax.numpy as jnp
from jax import lax
from jax.sharding import PartitionSpec as P

RHS = 8
ITERS = 3
HIGH = lax.Precision.HIGHEST


def with_halo(block, sides, width):
    for axis, dim in sides:
        count = lax.axis_size(axis)
        forward = [(i, i + 1) for i in range(count - 1)]
        backward = [(target, source) for source, target in forward]
        low = lax.ppermute(
            lax.slice_in_dim(block, block.shape[dim] - width, None, axis=dim), axis, forward
        )
        high = lax.ppermute(lax.slice_in_dim(block, 0, width, axis=dim), axis, backward)
        block = jnp.concatenate([low, block, high], axis=dim)
    return block


def couple(padded, blocks):
    views = [
        padded[:, :, 1:-1, 1:-1, 1:-1],
        padded[:, :, 2:, 1:-1, 1:-1],
        padded[:, :, :-2, 1:-1, 1:-1],
        padded[:, :, 1:-1, 2:, 1:-1],
        padded[:, :, 1:-1, :-2, 1:-1],
        padded[:, :, 1:-1, 1:-1, 2:],
        padded[:, :, 1:-1, 1:-1, :-2],
    ]
    total = jnp.zeros(views[0].shape, jnp.float32)
    for k in range(7):
        for j in range(views[0].shape[0]):
            column = blocks[k, :, j].astype(jnp.float32)
            total = total + column[:, None] * views[k][j][None]
    return total


def stencil(field, blocks):
    padded = with_halo(field, (("gx", 2), ("gy", 3), ("gz", 4)), 1)
    return couple(padded, blocks)


def pair(first, second):
    return jnp.einsum("arxyz,asxyz->rs", first, second, precision=HIGH)


def mix(field, matrix):
    return jnp.einsum("asxyz,sr->arxyz", field, matrix, precision=HIGH)


def normalizer(gram, eye):
    lower = jnp.linalg.cholesky(gram)
    inverse = lax.linalg.triangular_solve(lower, eye, left_side=True, lower=True)
    return (inverse.T, lower.T)


def shards(rhs, blocks):
    eye = jnp.eye(RHS, dtype=jnp.float32)
    hess = jnp.zeros((ITERS + 1, RHS, ITERS, RHS), jnp.float32)
    first_pair = None
    raw_image = stencil(rhs, blocks)
    gram_start, cross, square = lax.psum(
        (pair(rhs, rhs), pair(rhs, raw_image), pair(raw_image, raw_image)), ("gx", "gy", "gz")
    )
    scale, upper = normalizer(gram_start, eye)
    basis = [mix(rhs, scale)]
    images = [mix(raw_image, scale)]
    first_coeff = jnp.dot(jnp.dot(scale.T, cross, precision=HIGH), scale, precision=HIGH)
    first_gram = jnp.dot(jnp.dot(scale.T, square, precision=HIGH), scale, precision=HIGH)
    first_pair = (first_coeff, first_gram)
    for step in range(ITERS):
        image = images[step]
        if step == 0 and first_pair is not None:
            coeffs = [first_pair[0]]
            gram = first_pair[1]
        else:
            stacked = jnp.stack(basis + [image])
            partial_sums = jnp.einsum("karxyz,asxyz->krs", stacked, image, precision=HIGH)
            summed = lax.psum(partial_sums, ("gx", "gy", "gz"))
            coeffs = [summed[index] for index in range(len(basis))]
            gram = summed[len(basis)]
        rest = image
        for vector, coeff in zip(basis, coeffs):
            gram = gram - jnp.dot(coeff.T, coeff, precision=HIGH)
            rest = rest - mix(vector, coeff)
        scale, upper = normalizer(gram, eye)
        fresh = mix(rest, scale)
        basis.append(fresh)
        for index, coeff in enumerate(coeffs):
            hess = hess.at[index, :, step, :].set(coeff)
        hess = hess.at[step + 1, :, step, :].set(upper)
        if step + 1 < ITERS:
            images.append(stencil(fresh, blocks))
    return (jnp.stack(basis), hess)


def solution(mesh):
    placed = (P(None, None, "gx", "gy", "gz"), P(None, None, None, "gx", "gy", "gz"))
    return jax.shard_map(
        shards,
        mesh=mesh,
        in_specs=placed,
        out_specs=(P(None, None, None, "gx", "gy", "gz"), P()),
        check_vma=False,
    )
```

profile of v0, /device:TPU:0, one launch (start us, length us, event | category | flops | bytes accessed | tf_op | source)
XLA Modules:
  0.0 246.0 jit_solution(17078392354189909345)
XLA Ops:
  0.6 1.0 copy.203
  1.6 4.9 %collective-permute-start.1 = (f32[8,8,1,4,128]{4,1,3,2,0:T(8,128)S(1)}, f32[8,8,1,4,128]{4,1,3,2,0:T(8,128)S(1)}, u32[]{:S(2)}, u32[]{:S(2)}) collective-permute-start(f32[8,8,1,4,128]{4,1,3,2,0:T(8,128)S(1)} %copy.203), channel_id=1, source_target_pairs={{0,16},{1,17},{2,18},{3,19},{4,20},{5,21},{6,22},{7,23},{8,24},{9,... | collective-permute-start | bytes 393224 | tf_op jit(solution)/shard_map/ppermute | solution.py:16
  6.5 1.3 collective-permute-start
  7.8 0.9 bitcast_convert_fusion.53
  10.2 3.1 %collective-permute-done = f32[8,8,1,4,128]{4,1,3,2,0:T(8,128)S(1)} collective-permute-done((f32[8,8,1,4,128]{4,1,3,2,0:T(8,128)S(1)}, f32[8,8,1,4,128]{4,1,3,2,0:T(8,128)S(1)}, u32[]{:S(2)}, u32[]{:S(2)}) %collective-permute-start) | collective-permute-done | bytes 131104 | tf_op jit(solution)/shard_map/ppermute | solution.py:19
  13.4 1.3 collective-permute-start.2
  14.7 3.0 %collective-permute-start.3 = (f32[8,8,3,1,128]{4,1,3,2,0:T(8,128)S(1)}, f32[8,8,3,1,128]{4,1,3,2,0:T(8,128)S(1)}, u32[]{:S(2)}, u32[]{:S(2)}) collective-permute-start(f32[8,8,3,1,128]{4,1,3,2,0:T(8,128)S(1)} %get-tuple-element.285), channel_id=1, source_target_pairs={{0,4},{4,8},{8,12},{1,5},{5,9},{9,13},{2,6},{6,10},{10,14},{3,7},{... | collective-permute-start | bytes 294920 | tf_op jit(solution)/shard_map/ppermute | solution.py:16
  18.9 0.9 copy.278
  19.8 3.5 %collective-permute-start.5 = (f32[8,8,3,6,1]{1,0,4,3,2:T(8,128)S(1)}, f32[8,8,3,6,1]{1,0,4,3,2:T(8,128)S(1)}, u32[]{:S(2)}, u32[]{:S(2)}) collective-permute-start(f32[8,8,3,6,1]{1,0,4,3,2:T(8,128)S(1)} %copy.278), channel_id=1, source_target_pairs={{0,1},{1,2},{2,3},{4,5},{5,6},{6,7},{8,9},{9,10},{10,11},{12,13},{... | collective-permute-start | bytes 13832 | tf_op jit(solution)/shard_map/ppermute | solution.py:16
  24.2 1.3 collective-permute-start.4
  25.6 0.9 copy.209
  26.7 4.0 %collective-permute-done.4 = f32[8,8,3,6,1]{1,0,4,3,2:T(8,128)S(1)} collective-permute-done((f32[8,8,3,6,1]{1,0,4,3,2:T(8,128)S(1)}, f32[8,8,3,6,1]{1,0,4,3,2:T(8,128)S(1)}, u32[]{:S(2)}, u32[]{:S(2)}) %collective-permute-start.4) | collective-permute-done | bytes 4640 | tf_op jit(solution)/shard_map/ppermute | solution.py:19
  30.7 0.9 copy.207
  31.8 1.0 multiply_add_fusion.2
  33.6 41.6 %all-reduce.1 = (f32[8,8]{0,1:T(8,128)S(1)}, f32[8,8]{1,0:T(8,128)S(1)}, f32[8,8]{0,1:T(8,128)S(1)}) all-reduce(f32[8,8]{0,1:T(8,128)S(1)} %convolution_bitcast_fusion.13, f32[8,8]{1,0:T(8,128)S(1)} %convolution_bitcast_fusion.12, f32[8,8]{0,1:T(8,128)S(1)} %convolution_bitcast_fusion.11), channel_id=1, replica_groups=mesh['gx'=2,'gy'=4,'gz'=4] {'gx','gy','gz'}, use_global_device_ids=true, to_apply=%region_0.0 | all-reduce | flops 192 | bytes 1536 | tf_op jit(solution)/shard_map/psum | solution.py:66
  83.0 1.3 collective-permute-start.6
  84.3 4.6 %collective-permute-start.7 = (f32[8,8,1,4,128]{4,1,3,0,2:T(8,128)S(1)}, f32[8,8,1,4,128]{4,1,3,0,2:T(8,128)S(1)}, u32[]{:S(2)}, u32[]{:S(2)}) collective-permute-start(f32[8,8,1,4,128]{4,1,3,0,2:T(8,128)S(1)} %bitcast.786), channel_id=1, source_target_pairs={{0,16},{1,17},{2,18},{3,19},{4,20},{5,21},{6,22},{7,23},{8,24},{9,... | collective-permute-start | bytes 393224 | tf_op jit(solution)/shard_map/ppermute | solution.py:16
  90.8 2.8 %and_reduce_fusion = (pred[]{:T(512)}, pred[]{:T(512)}) fusion(s32[4]{0:T(128)S(1)} %copy-done.3, s32[1]{0:T(128)} %constant.288.clone.1, s32[1]{0:T(128)} %get-tuple-element.366, s32[1]{0:T(128)} %get-tuple-element.365, s32[1]{0:T(128)} %slice.1472, s32[1]{0:T(128)S(1)} %bitcast.825), kind=kLoop, calls=%fused_computation.849 | loop fusion | flops 54 | bytes 38 | tf_op jit(solution)/shard_map/reduce.18
  93.7 1.3 collective-permute-start.8
  95.0 3.0 %collective-permute-start.9 = (f32[8,8,3,1,128]{4,1,3,0,2:T(8,128)S(1)}, f32[8,8,3,1,128]{4,1,3,0,2:T(8,128)S(1)}, u32[]{:S(2)}, u32[]{:S(2)}) collective-permute-start(f32[8,8,3,1,128]{4,1,3,0,2:T(8,128)S(1)} %get-tuple-element.283), channel_id=1, source_target_pairs={{0,4},{4,8},{8,12},{1,5},{5,9},{9,13},{2,6},{6,10},{10,14},{3,7},{... | collective-permute-start | bytes 294920 | tf_op jit(solution)/shard_map/ppermute | solution.py:16
  99.2 0.9 copy.218
  100.1 2.2 collective-permute-start.11
  103.2 1.3 collective-permute-start.10
  104.6 0.9 copy.219
  105.7 3.7 %collective-permute-done.10 = f32[8,8,3,6,1]{1,0,4,3,2:T(8,128)S(1)} collective-permute-done((f32[8,8,3,6,1]{1,0,4,3,2:T(8,128)S(1)}, f32[8,8,3,6,1]{1,0,4,3,2:T(8,128)S(1)}, u32[]{:S(2)}, u32[]{:S(2)}) %collective-permute-start.10) | collective-permute-done | bytes 4640 | tf_op jit(solution)/shard_map/ppermute | solution.py:19
  109.4 0.9 copy.217
  110.6 1.1 multiply_add_fusion.1
  111.7 1.6 convolution_bitcast_fusion.7
  113.3 42.8 %psum.38 = f32[3,8,8]{2,1,0:T(8,128)S(1)} all-reduce(f32[3,8,8]{2,1,0:T(8,128)S(1)} %convolution_bitcast_fusion.7), channel_id=1, replica_groups=mesh['gx'=2,'gy'=4,'gz'=4] {'gx','gy','gz'}, use_global_device_ids=true, to_apply=%region_5.8 | all-reduce | flops 192 | bytes 1536 | tf_op jit(solution)/shard_map/psum | solution.py:83
  159.8 1.3 fusion.3
  161.4 1.3 collective-permute-start.12
  162.7 4.6 %collective-permute-start.13 = (f32[8,8,1,4,128]{4,1,3,0,2:T(8,128)S(1)}, f32[8,8,1,4,128]{4,1,3,0,2:T(8,128)S(1)}, u32[]{:S(2)}, u32[]{:S(2)}) collective-permute-start(f32[8,8,1,4,128]{4,1,3,0,2:T(8,128)S(1)} %bitcast.803), channel_id=1, source_target_pairs={{0,16},{1,17},{2,18},{3,19},{4,20},{5,21},{6,22},{7,23},{8,24},{9,... | collective-permute-start | bytes 393224 | tf_op jit(solution)/shard_map/ppermute | solution.py:16
  167.3 1.3 fusion.499
  168.7 1.1 collective-permute-done.13
  169.8 1.3 collective-permute-start.14
  171.1 3.0 %collective-permute-start.15 = (f32[8,8,3,1,128]{4,1,3,0,2:T(8,128)S(1)}, f32[8,8,3,1,128]{4,1,3,0,2:T(8,128)S(1)}, u32[]{:S(2)}, u32[]{:S(2)}) collective-permute-start(f32[8,8,3,1,128]{4,1,3,0,2:T(8,128)S(1)} %get-tuple-element.281), channel_id=1, source_target_pairs={{0,4},{4,8},{8,12},{1,5},{5,9},{9,13},{2,6},{6,10},{10,14},{3,7},{... | collective-permute-start | bytes 294920 | tf_op jit(solution)/shard_map/ppermute | solution.py:16
  175.3 0.9 copy.230
  176.2 2.2 collective-permute-start.17
  179.3 1.3 collective-permute-start.16
  180.7 0.9 copy.231
  181.8 3.7 %collective-permute-done.16 = f32[8,8,3,6,1]{1,0,4,3,2:T(8,128)S(1)} collective-permute-done((f32[8,8,3,6,1]{1,0,4,3,2:T(8,128)S(1)}, f32[8,8,3,6,1]{1,0,4,3,2:T(8,128)S(1)}, u32[]{:S(2)}, u32[]{:S(2)}) %collective-permute-start.16) | collective-permute-done | bytes 4640 | tf_op jit(solution)/shard_map/ppermute | solution.py:19
  185.5 0.9 copy.229
  186.7 1.0 multiply_add_fusion
  187.8 1.6 convolution_bitcast_fusion.6
  189.4 44.9 %psum.39 = f32[4,8,8]{2,1,0:T(8,128)S(1)} all-reduce(f32[4,8,8]{2,1,0:T(8,128)S(1)} %convolution_bitcast_fusion.6), channel_id=1, replica_groups=mesh['gx'=2,'gy'=4,'gz'=4] {'gx','gy','gz'}, use_global_device_ids=true, to_apply=%region_6.9 | all-reduce | flops 256 | bytes 2048 | tf_op jit(solution)/shard_map/psum | solution.py:83
  238.6 1.1 fusion.7
  240.0 0.9 copy.245
  240.9 3.3 %fusion.498 = f32[4,8,3,8]{3,1,2,0:T(8,128)} fusion(f32[4,8,3,8]{3,1,2,0:T(8,128)} %copy-done.2, s32[]{:T(128)} %bitcast.379, s32[]{:T(128)} %bitcast.380, f32[4,8,8]{2,1,0:T(8,128)S(1)} %psum.39, pred[]{:T(512)} %get-tuple-element.118), kind=kLoop, calls=%fused_computation.797 | loop fusion | flops 64 | bytes 9984 | tf_op jit(solution)/shard_map/scatter | solution.py:94
  (149 shorter events, 30.1 us)
Async XLA Ops:
  0.6 8.1 %copy-start.1 = (bf16[7,8,8,1,4,128]{5,4,3,2,1,0:T(4,128)(2,1)S(1)}, bf16[7,8,8,1,4,128]{5,4,3,2,1,0:T(4,128)(2,1)}, u32[]{:S(2)}) copy-start(bf16[7,8,8,1,4,128]{5,4,3,2,1,0:T(4,128)(2,1)} %param.24) | copy-start | bytes 1376260
  1.6 8.5 %collective-permute-start.1 = (f32[8,8,1,4,128]{4,1,3,2,0:T(8,128)S(1)}, f32[8,8,1,4,128]{4,1,3,2,0:T(8,128)S(1)}, u32[]{:S(2)}, u32[]{:S(2)}) collective-permute-start(f32[8,8,1,4,128]{4,1,3,2,0:T(8,128)S(1)} %copy.203), channel_id=1, source_target_pairs={{0,16},{1,17},{2,18},{3,19},{4,20},{5,21},{6,22},{7,23},{8,24},{9,... | collective-permute-start | bytes 393224 | tf_op jit(solution)/shard_map/ppermute | solution.py:16
  6.5 6.9 %collective-permute-start = (f32[8,8,1,4,128]{4,1,3,2,0:T(8,128)S(1)}, f32[8,8,1,4,128]{4,1,3,2,0:T(8,128)S(1)}, u32[]{:S(2)}, u32[]{:S(2)}) collective-permute-start(f32[8,8,1,4,128]{4,1,3,2,0:T(8,128)S(1)} %copy.203), channel_id=1, source_target_pairs={{16,0},{17,1},{18,2},{19,3},{20,4},{21,5},{22,6},{23,7},{24,8},{25... | collective-permute-start | bytes 393224 | tf_op jit(solution)/shard_map/ppermute | solution.py:19
  8.8 0.9 copy-start
  13.4 4.4 %collective-permute-start.2 = (f32[8,8,3,1,128]{4,1,3,2,0:T(8,128)S(1)}, f32[8,8,3,1,128]{4,1,3,2,0:T(8,128)S(1)}, u32[]{:S(2)}, u32[]{:S(2)}) collective-permute-start(f32[8,8,3,1,128]{4,1,3,2,0:T(8,128)S(1)} %get-tuple-element.286), channel_id=1, source_target_pairs={{4,0},{8,4},{12,8},{5,1},{9,5},{13,9},{6,2},{10,6},{14,10},{7,3},{... | collective-permute-start | bytes 294920 | tf_op jit(solution)/shard_map/ppermute | solution.py:19
  14.7 4.0 %collective-permute-start.3 = (f32[8,8,3,1,128]{4,1,3,2,0:T(8,128)S(1)}, f32[8,8,3,1,128]{4,1,3,2,0:T(8,128)S(1)}, u32[]{:S(2)}, u32[]{:S(2)}) collective-permute-start(f32[8,8,3,1,128]{4,1,3,2,0:T(8,128)S(1)} %get-tuple-element.285), channel_id=1, source_target_pairs={{0,4},{4,8},{8,12},{1,5},{5,9},{9,13},{2,6},{6,10},{10,14},{3,7},{... | collective-permute-start | bytes 294920 | tf_op jit(solution)/shard_map/ppermute | solution.py:16
  19.8 5.7 %collective-permute-start.5 = (f32[8,8,3,6,1]{1,0,4,3,2:T(8,128)S(1)}, f32[8,8,3,6,1]{1,0,4,3,2:T(8,128)S(1)}, u32[]{:S(2)}, u32[]{:S(2)}) collective-permute-start(f32[8,8,3,6,1]{1,0,4,3,2:T(8,128)S(1)} %copy.278), channel_id=1, source_target_pairs={{0,1},{1,2},{2,3},{4,5},{5,6},{6,7},{8,9},{9,10},{10,11},{12,13},{... | collective-permute-start | bytes 13832 | tf_op jit(solution)/shard_map/ppermute | solution.py:16
  24.2 6.5 %collective-permute-start.4 = (f32[8,8,3,6,1]{1,0,4,3,2:T(8,128)S(1)}, f32[8,8,3,6,1]{1,0,4,3,2:T(8,128)S(1)}, u32[]{:S(2)}, u32[]{:S(2)}) collective-permute-start(f32[8,8,3,6,1]{1,0,4,3,2:T(8,128)S(1)} %copy.277), channel_id=1, source_target_pairs={{1,0},{2,1},{3,2},{5,4},{6,5},{7,6},{9,8},{10,9},{11,10},{13,12},{... | collective-permute-start | bytes 13832 | tf_op jit(solution)/shard_map/ppermute | solution.py:19
  83.0 10.6 %collective-permute-start.6 = (f32[8,8,1,4,128]{4,1,3,0,2:T(8,128)S(1)}, f32[8,8,1,4,128]{4,1,3,0,2:T(8,128)S(1)}, u32[]{:S(2)}, u32[]{:S(2)}) collective-permute-start(f32[8,8,1,4,128]{4,1,3,0,2:T(8,128)S(1)} %bitcast.785), channel_id=1, source_target_pairs={{16,0},{17,1},{18,2},{19,3},{20,4},{21,5},{22,6},{23,7},{24,8},{25... | collective-permute-start | bytes 393224 | tf_op jit(solution)/shard_map/ppermute | solution.py:19
  84.3 9.3 %collective-permute-start.7 = (f32[8,8,1,4,128]{4,1,3,0,2:T(8,128)S(1)}, f32[8,8,1,4,128]{4,1,3,0,2:T(8,128)S(1)}, u32[]{:S(2)}, u32[]{:S(2)}) collective-permute-start(f32[8,8,1,4,128]{4,1,3,0,2:T(8,128)S(1)} %bitcast.786), channel_id=1, source_target_pairs={{0,16},{1,17},{2,18},{3,19},{4,20},{5,21},{6,22},{7,23},{8,24},{9,... | collective-permute-start | bytes 393224 | tf_op jit(solution)/shard_map/ppermute | solution.py:16
  90.1 0.7 copy-start.3
  93.7 4.4 %collective-permute-start.8 = (f32[8,8,3,1,128]{4,1,3,0,2:T(8,128)S(1)}, f32[8,8,3,1,128]{4,1,3,0,2:T(8,128)S(1)}, u32[]{:S(2)}, u32[]{:S(2)}) collective-permute-start(f32[8,8,3,1,128]{4,1,3,0,2:T(8,128)S(1)} %get-tuple-element.284), channel_id=1, source_target_pairs={{4,0},{8,4},{12,8},{5,1},{9,5},{13,9},{6,2},{10,6},{14,10},{7,3},{... | collective-permute-start | bytes 294920 | tf_op jit(solution)/shard_map/ppermute | solution.py:19
  95.0 4.0 %collective-permute-start.9 = (f32[8,8,3,1,128]{4,1,3,0,2:T(8,128)S(1)}, f32[8,8,3,1,128]{4,1,3,0,2:T(8,128)S(1)}, u32[]{:S(2)}, u32[]{:S(2)}) collective-permute-start(f32[8,8,3,1,128]{4,1,3,0,2:T(8,128)S(1)} %get-tuple-element.283), channel_id=1, source_target_pairs={{0,4},{4,8},{8,12},{1,5},{5,9},{9,13},{2,6},{6,10},{10,14},{3,7},{... | collective-permute-start | bytes 294920 | tf_op jit(solution)/shard_map/ppermute | solution.py:16
  100.1 4.5 %collective-permute-start.11 = (f32[8,8,3,6,1]{1,0,4,3,2:T(8,128)S(1)}, f32[8,8,3,6,1]{1,0,4,3,2:T(8,128)S(1)}, u32[]{:S(2)}, u32[]{:S(2)}) collective-permute-start(f32[8,8,3,6,1]{1,0,4,3,2:T(8,128)S(1)} %copy.218), channel_id=1, source_target_pairs={{0,1},{1,2},{2,3},{4,5},{5,6},{6,7},{8,9},{9,10},{10,11},{12,13},{... | collective-permute-start | bytes 13832 | tf_op jit(solution)/shard_map/ppermute | solution.py:16
  103.2 6.2 %collective-permute-start.10 = (f32[8,8,3,6,1]{1,0,4,3,2:T(8,128)S(1)}, f32[8,8,3,6,1]{1,0,4,3,2:T(8,128)S(1)}, u32[]{:S(2)}, u32[]{:S(2)}) collective-permute-start(f32[8,8,3,6,1]{1,0,4,3,2:T(8,128)S(1)} %copy.216), channel_id=1, source_target_pairs={{1,0},{2,1},{3,2},{5,4},{6,5},{7,6},{9,8},{10,9},{11,10},{13,12},{... | collective-permute-start | bytes 13832 | tf_op jit(solution)/shard_map/ppermute | solution.py:19
  161.4 7.3 %collective-permute-start.12 = (f32[8,8,1,4,128]{4,1,3,0,2:T(8,128)S(1)}, f32[8,8,1,4,128]{4,1,3,0,2:T(8,128)S(1)}, u32[]{:S(2)}, u32[]{:S(2)}) collective-permute-start(f32[8,8,1,4,128]{4,1,3,0,2:T(8,128)S(1)} %bitcast.802), channel_id=1, source_target_pairs={{16,0},{17,1},{18,2},{19,3},{20,4},{21,5},{22,6},{23,7},{24,8},{25... | collective-permute-start | bytes 393224 | tf_op jit(solution)/shard_map/ppermute | solution.py:19
  162.7 7.1 %collective-permute-start.13 = (f32[8,8,1,4,128]{4,1,3,0,2:T(8,128)S(1)}, f32[8,8,1,4,128]{4,1,3,0,2:T(8,128)S(1)}, u32[]{:S(2)}, u32[]{:S(2)}) collective-permute-start(f32[8,8,1,4,128]{4,1,3,0,2:T(8,128)S(1)} %bitcast.803), channel_id=1, source_target_pairs={{0,16},{1,17},{2,18},{3,19},{4,20},{5,21},{6,22},{7,23},{8,24},{9,... | collective-permute-start | bytes 393224 | tf_op jit(solution)/shard_map/ppermute | solution.py:16
  169.8 4.4 %collective-permute-start.14 = (f32[8,8,3,1,128]{4,1,3,0,2:T(8,128)S(1)}, f32[8,8,3,1,128]{4,1,3,0,2:T(8,128)S(1)}, u32[]{:S(2)}, u32[]{:S(2)}) collective-permute-start(f32[8,8,3,1,128]{4,1,3,0,2:T(8,128)S(1)} %get-tuple-element.282), channel_id=1, source_target_pairs={{4,0},{8,4},{12,8},{5,1},{9,5},{13,9},{6,2},{10,6},{14,10},{7,3},{... | collective-permute-start | bytes 294920 | tf_op jit(solution)/shard_map/ppermute | solution.py:19
  171.1 4.0 %collective-permute-start.15 = (f32[8,8,3,1,128]{4,1,3,0,2:T(8,128)S(1)}, f32[8,8,3,1,128]{4,1,3,0,2:T(8,128)S(1)}, u32[]{:S(2)}, u32[]{:S(2)}) collective-permute-start(f32[8,8,3,1,128]{4,1,3,0,2:T(8,128)S(1)} %get-tuple-element.281), channel_id=1, source_target_pairs={{0,4},{4,8},{8,12},{1,5},{5,9},{9,13},{2,6},{6,10},{10,14},{3,7},{... | collective-permute-start | bytes 294920 | tf_op jit(solution)/shard_map/ppermute | solution.py:16
  174.1 0.9 copy-start.2
  176.2 4.5 %collective-permute-start.17 = (f32[8,8,3,6,1]{1,0,4,3,2:T(8,128)S(1)}, f32[8,8,3,6,1]{1,0,4,3,2:T(8,128)S(1)}, u32[]{:S(2)}, u32[]{:S(2)}) collective-permute-start(f32[8,8,3,6,1]{1,0,4,3,2:T(8,128)S(1)} %copy.230), channel_id=1, source_target_pairs={{0,1},{1,2},{2,3},{4,5},{5,6},{6,7},{8,9},{9,10},{10,11},{12,13},{... | collective-permute-start | bytes 13832 | tf_op jit(solution)/shard_map/ppermute | solution.py:16
  179.3 6.2 %collective-permute-start.16 = (f32[8,8,3,6,1]{1,0,4,3,2:T(8,128)S(1)}, f32[8,8,3,6,1]{1,0,4,3,2:T(8,128)S(1)}, u32[]{:S(2)}, u32[]{:S(2)}) collective-permute-start(f32[8,8,3,6,1]{1,0,4,3,2:T(8,128)S(1)} %copy.228), channel_id=1, source_target_pairs={{1,0},{2,1},{3,2},{5,4},{6,5},{7,6},{9,8},{10,9},{11,10},{13,12},{... | collective-permute-start | bytes 13832 | tf_op jit(solution)/shard_map/ppermute | solution.py:19
where the time goes:
time: 247 us; the launch traced here: 246 us
  blocking collectives  129 us (52%)
  starting transfers between devices  42.5 us (17%)
  other arithmetic  23.9 us (10%)
  local copies, waits for them, and re-layouts  18.8 us (8%)
  waiting for transfers between devices  18.3 us (7%)
  matrix products  11.8 us (5%)
    psum x2, blocking collectives, shards(): summed = lax.psum(partial_sums, ('gx', 'gy', 'gz'))  87.7 us
    psum x1, blocking collectives, shards(): lax.psum((pair(rhs, rhs), pair(rhs, raw_image), pair(raw_image, raw_image...  41.6 us
    ppermute x9, starting transfers between devices, with_halo(): lax.ppermute(lax.slice_in_dim(block, block.shape[dim] - width, None, axis...  30.9 us
    ppermute x9, waiting for transfers between devices, with_halo(): lax.ppermute(lax.slice_in_dim(block, 0, width, axis=dim), axis, backward)  14.6 us
    ppermute x9, starting transfers between devices, with_halo(): lax.ppermute(lax.slice_in_dim(block, 0, width, axis=dim), axis, backward)  11.6 us
    another operation x12, other arithmetic, normalizer(): lower = jnp.linalg.cholesky(gram)  5.63 us
    unnamed x14, local copies, waits for them, and re-layouts  5.27 us
    dot_general x11, matrix products, mix(): return jnp.einsum('asxyz,sr->arxyz', field, matrix, precision=HIGH)  4.97 us
  transfers between devices with their start and end apart: 18, of which 8 were waited for; matrix products, arithmetic and copies ran while one was open for 5% of the time, Pallas kernels for 0%

commit v1 on v0

--- a/solution.py
+++ b/solution.py
@@ -80,7 +80,7 @@
         else:
             stacked = jnp.stack(basis + [image])
             partial_sums = jnp.einsum("karxyz,asxyz->krs", stacked, image, precision=HIGH)
-            summed = lax.psum(partial_sums, ("gx", "gy", "gz"))
+            summed = jnp.sum(lax.all_gather(partial_sums, ("gx", "gy", "gz")), axis=0)
             coeffs = [summed[index] for index in range(len(basis))]
             gram = summed[len(basis)]
         rest = image

time: 247 us -> 296 us (1.20)
  blocking collectives: 129 us -> 178 us
    all_gather x0 -> x2, blocking collectives: none -> 137 us  [shards(): summed = jnp.sum(lax.all_gather(partial_sums, ('gx', 'gy', 'gz')), axis=0)]
    psum x2 -> x0, blocking collectives: 87.7 us -> none  [shards(): summed = lax.psum(partial_sums, ('gx', 'gy', 'gz'))]
  transfers between devices with their start and end apart: 18 -> 18, of which waited for: 8 -> 9; matrix products, arithmetic and copies ran while one was open for 5% -> 4% of each run, Pallas kernels for 0% -> 0%
where the time goes in v1:
time: 296 us
  blocking collectives  178 us (60%)
  starting transfers between devices  42.7 us (14%)
  other arithmetic  24 us (8%)
  local copies, waits for them, and re-layouts  18.8 us (6%)
  waiting for transfers between devices  18.6 us (6%)
  matrix products  11.8 us (4%)
    all_gather x2, blocking collectives, shards(): summed = jnp.sum(lax.all_gather(partial_sums, ('gx', 'gy', 'gz')), axis=0)  137 us
    psum x1, blocking collectives, shards(): lax.psum((pair(rhs, rhs), pair(rhs, raw_image), pair(raw_image, raw_image...  41.6 us
    ppermute x9, starting transfers between devices, with_halo(): lax.ppermute(lax.slice_in_dim(block, block.shape[dim] - width, None, axis...  31.1 us
    ppermute x9, waiting for transfers between devices, with_halo(): lax.ppermute(lax.slice_in_dim(block, 0, width, axis=dim), axis, backward)  14.7 us
    ppermute x9, starting transfers between devices, with_halo(): lax.ppermute(lax.slice_in_dim(block, 0, width, axis=dim), axis, backward)  11.6 us
  transfers between devices with their start and end apart: 18, of which 9 were waited for; matrix products, arithmetic and copies ran while one was open for 4% of the time, Pallas kernels for 0%

profile of v1, /device:TPU:0, one launch (start us, length us, event | category | flops | bytes accessed | tf_op | source)
XLA Modules:
  0.0 295.6 jit_solution(8107745335727928824)
XLA Ops:
  0.6 1.0 copy.203
  1.6 4.9 %collective-permute-start.1 = (f32[8,8,1,4,128]{4,1,3,2,0:T(8,128)S(1)}, f32[8,8,1,4,128]{4,1,3,2,0:T(8,128)S(1)}, u32[]{:S(2)}, u32[]{:S(2)}) collective-permute-start(f32[8,8,1,4,128]{4,1,3,2,0:T(8,128)S(1)} %copy.203), channel_id=1, source_target_pairs={{0,16},{1,17},{2,18},{3,19},{4,20},{5,21},{6,22},{7,23},{8,24},{9,... | collective-permute-start | bytes 393224 | tf_op jit(solution)/shard_map/ppermute | solution.py:16
  6.5 1.3 collective-permute-start
  7.8 0.9 bitcast_convert_fusion.53
  10.2 3.1 %collective-permute-done = f32[8,8,1,4,128]{4,1,3,2,0:T(8,128)S(1)} collective-permute-done((f32[8,8,1,4,128]{4,1,3,2,0:T(8,128)S(1)}, f32[8,8,1,4,128]{4,1,3,2,0:T(8,128)S(1)}, u32[]{:S(2)}, u32[]{:S(2)}) %collective-permute-start) | collective-permute-done | bytes 131104 | tf_op jit(solution)/shard_map/ppermute | solution.py:19
  13.4 1.3 collective-permute-start.2
  14.7 3.0 %collective-permute-start.3 = (f32[8,8,3,1,128]{4,1,3,2,0:T(8,128)S(1)}, f32[8,8,3,1,128]{4,1,3,2,0:T(8,128)S(1)}, u32[]{:S(2)}, u32[]{:S(2)}) collective-permute-start(f32[8,8,3,1,128]{4,1,3,2,0:T(8,128)S(1)} %get-tuple-element.285), channel_id=1, source_target_pairs={{0,4},{4,8},{8,12},{1,5},{5,9},{9,13},{2,6},{6,10},{10,14},{3,7},{... | collective-permute-start | bytes 294920 | tf_op jit(solution)/shard_map/ppermute | solution.py:16
  18.9 0.9 copy.278
  19.8 3.5 %collective-permute-start.5 = (f32[8,8,3,6,1]{1,0,4,3,2:T(8,128)S(1)}, f32[8,8,3,6,1]{1,0,4,3,2:T(8,128)S(1)}, u32[]{:S(2)}, u32[]{:S(2)}) collective-permute-start(f32[8,8,3,6,1]{1,0,4,3,2:T(8,128)S(1)} %copy.278), channel_id=1, source_target_pairs={{0,1},{1,2},{2,3},{4,5},{5,6},{6,7},{8,9},{9,10},{10,11},{12,13},{... | collective-permute-start | bytes 13832 | tf_op jit(solution)/shard_map/ppermute | solution.py:16
  24.2 1.3 collective-permute-start.4
  25.6 0.9 copy.209
  26.7 4.0 %collective-permute-done.4 = f32[8,8,3,6,1]{1,0,4,3,2:T(8,128)S(1)} collective-permute-done((f32[8,8,3,6,1]{1,0,4,3,2:T(8,128)S(1)}, f32[8,8,3,6,1]{1,0,4,3,2:T(8,128)S(1)}, u32[]{:S(2)}, u32[]{:S(2)}) %collective-permute-start.4) | collective-permute-done | bytes 4640 | tf_op jit(solution)/shard_map/ppermute | solution.py:19
  30.7 0.9 copy.207
  31.8 1.0 multiply_add_fusion.2
  33.6 41.6 %all-reduce.1 = (f32[8,8]{0,1:T(8,128)S(1)}, f32[8,8]{1,0:T(8,128)S(1)}, f32[8,8]{0,1:T(8,128)S(1)}) all-reduce(f32[8,8]{0,1:T(8,128)S(1)} %convolution_bitcast_fusion.13, f32[8,8]{1,0:T(8,128)S(1)} %convolution_bitcast_fusion.12, f32[8,8]{0,1:T(8,128)S(1)} %convolution_bitcast_fusion.11), channel_id=1, replica_groups=mesh['gx'=2,'gy'=4,'gz'=4] {'gx','gy','gz'}, use_global_device_ids=true, to_apply=%region_0.0 | all-reduce | flops 192 | bytes 1536 | tf_op jit(solution)/shard_map/psum | solution.py:66
  83.0 1.3 collective-permute-start.6
  84.3 4.6 %collective-permute-start.7 = (f32[8,8,1,4,128]{4,1,3,0,2:T(8,128)S(1)}, f32[8,8,1,4,128]{4,1,3,0,2:T(8,128)S(1)}, u32[]{:S(2)}, u32[]{:S(2)}) collective-permute-start(f32[8,8,1,4,128]{4,1,3,0,2:T(8,128)S(1)} %bitcast.788), channel_id=1, source_target_pairs={{0,16},{1,17},{2,18},{3,19},{4,20},{5,21},{6,22},{7,23},{8,24},{9,... | collective-permute-start | bytes 393224 | tf_op jit(solution)/shard_map/ppermute | solution.py:16
  90.8 2.8 and_reduce_fusion
  93.7 1.3 collective-permute-start.8
  95.0 3.0 %collective-permute-start.9 = (f32[8,8,3,1,128]{4,1,3,0,2:T(8,128)S(1)}, f32[8,8,3,1,128]{4,1,3,0,2:T(8,128)S(1)}, u32[]{:S(2)}, u32[]{:S(2)}) collective-permute-start(f32[8,8,3,1,128]{4,1,3,0,2:T(8,128)S(1)} %get-tuple-element.283), channel_id=1, source_target_pairs={{0,4},{4,8},{8,12},{1,5},{5,9},{9,13},{2,6},{6,10},{10,14},{3,7},{... | collective-permute-start | bytes 294920 | tf_op jit(solution)/shard_map/ppermute | solution.py:16
  99.2 0.9 copy.218
  100.1 2.2 collective-permute-start.11
  103.2 1.3 collective-permute-start.10
  104.6 0.9 copy.219
  105.7 3.7 %collective-permute-done.10 = f32[8,8,3,6,1]{1,0,4,3,2:T(8,128)S(1)} collective-permute-done((f32[8,8,3,6,1]{1,0,4,3,2:T(8,128)S(1)}, f32[8,8,3,6,1]{1,0,4,3,2:T(8,128)S(1)}, u32[]{:S(2)}, u32[]{:S(2)}) %collective-permute-start.10) | collective-permute-done | bytes 4640 | tf_op jit(solution)/shard_map/ppermute | solution.py:19
  109.4 0.9 copy.217
  110.6 1.1 multiply_add_fusion.1
  111.7 1.6 convolution_bitcast_fusion.7
  113.3 68.6 %all-gather = f32[96,8,8]{2,1,0:T(8,128)S(1)} all-gather(f32[3,8,8]{2,1,0:T(8,128)S(1)} %convolution_bitcast_fusion.7), channel_id=2, replica_groups=mesh['gx'=2,'gy'=4,'gz'=4] {'gx','gy','gz'}, dimensions={0}, use_global_device_ids=true | all-gather | bytes 25344 | tf_op jit(solution)/shard_map/all_gather | solution.py:83
  185.7 1.3 fusion.3
  187.2 1.3 collective-permute-start.12
  188.5 4.6 %collective-permute-start.13 = (f32[8,8,1,4,128]{4,1,3,0,2:T(8,128)S(1)}, f32[8,8,1,4,128]{4,1,3,0,2:T(8,128)S(1)}, u32[]{:S(2)}, u32[]{:S(2)}) collective-permute-start(f32[8,8,1,4,128]{4,1,3,0,2:T(8,128)S(1)} %bitcast.805), channel_id=1, source_target_pairs={{0,16},{1,17},{2,18},{3,19},{4,20},{5,21},{6,22},{7,23},{8,24},{9,... | collective-permute-start | bytes 393224 | tf_op jit(solution)/shard_map/ppermute | solution.py:16
  193.2 1.3 fusion.499
  194.5 1.1 collective-permute-done.13
  195.6 1.3 collective-permute-start.14
  196.9 3.0 %collective-permute-start.15 = (f32[8,8,3,1,128]{4,1,3,0,2:T(8,128)S(1)}, f32[8,8,3,1,128]{4,1,3,0,2:T(8,128)S(1)}, u32[]{:S(2)}, u32[]{:S(2)}) collective-permute-start(f32[8,8,3,1,128]{4,1,3,0,2:T(8,128)S(1)} %get-tuple-element.281), channel_id=1, source_target_pairs={{0,4},{4,8},{8,12},{1,5},{5,9},{9,13},{2,6},{6,10},{10,14},{3,7},{... | collective-permute-start | bytes 294920 | tf_op jit(solution)/shard_map/ppermute | solution.py:16
  201.1 0.9 copy.230
  202.0 2.3 collective-permute-start.17
  205.3 1.3 collective-permute-start.16
  206.7 0.9 copy.231
  207.9 3.9 %collective-permute-done.16 = f32[8,8,3,6,1]{1,0,4,3,2:T(8,128)S(1)} collective-permute-done((f32[8,8,3,6,1]{1,0,4,3,2:T(8,128)S(1)}, f32[8,8,3,6,1]{1,0,4,3,2:T(8,128)S(1)}, u32[]{:S(2)}, u32[]{:S(2)}) %collective-permute-start.16) | collective-permute-done | bytes 4640 | tf_op jit(solution)/shard_map/ppermute | solution.py:19
  211.8 0.9 copy.229
  213.0 1.0 multiply_add_fusion
  214.0 1.6 convolution_bitcast_fusion.6
  215.6 68.1 %all-gather.1 = f32[128,8,8]{2,1,0:T(8,128)S(1)} all-gather(f32[4,8,8]{2,1,0:T(8,128)S(1)} %convolution_bitcast_fusion.6), channel_id=3, replica_groups=mesh['gx'=2,'gy'=4,'gz'=4] {'gx','gy','gz'}, dimensions={0}, use_global_device_ids=true | all-gather | bytes 33792 | tf_op jit(solution)/shard_map/all_gather | solution.py:83
  288.1 1.1 fusion.7
  289.6 0.9 copy.245
  290.5 3.3 %fusion.498 = f32[4,8,3,8]{3,1,2,0:T(8,128)} fusion(f32[4,8,3,8]{3,1,2,0:T(8,128)} %copy-done.2, s32[]{:T(128)} %bitcast.381, s32[]{:T(128)} %bitcast.382, f32[4,8,8]{2,1,0:T(8,128)S(1)} %reduce_sum.19, pred[]{:T(512)} %get-tuple-element.118), kind=kLoop, calls=%fused_computation.797 | loop fusion | flops 64 | bytes 9984 | tf_op jit(solution)/shard_map/scatter | solution.py:94
  (151 shorter events, 30.3 us)
Async XLA Ops:
  0.6 8.1 %copy-start.1 = (bf16[7,8,8,1,4,128]{5,4,3,2,1,0:T(4,128)(2,1)S(1)}, bf16[7,8,8,1,4,128]{5,4,3,2,1,0:T(4,128)(2,1)}, u32[]{:S(2)}) copy-start(bf16[7,8,8,1,4,128]{5,4,3,2,1,0:T(4,128)(2,1)} %param.24) | copy-start | bytes 1376260
  1.6 8.5 %collective-permute-start.1 = (f32[8,8,1,4,128]{4,1,3,2,0:T(8,128)S(1)}, f32[8,8,1,4,128]{4,1,3,2,0:T(8,128)S(1)}, u32[]{:S(2)}, u32[]{:S(2)}) collective-permute-start(f32[8,8,1,4,128]{4,1,3,2,0:T(8,128)S(1)} %copy.203), channel_id=1, source_target_pairs={{0,16},{1,17},{2,18},{3,19},{4,20},{5,21},{6,22},{7,23},{8,24},{9,... | collective-permute-start | bytes 393224 | tf_op jit(solution)/shard_map/ppermute | solution.py:16
  6.5 6.9 %collective-permute-start = (f32[8,8,1,4,128]{4,1,3,2,0:T(8,128)S(1)}, f32[8,8,1,4,128]{4,1,3,2,0:T(8,128)S(1)}, u32[]{:S(2)}, u32[]{:S(2)}) collective-permute-start(f32[8,8,1,4,128]{4,1,3,2,0:T(8,128)S(1)} %copy.203), channel_id=1, source_target_pairs={{16,0},{17,1},{18,2},{19,3},{20,4},{21,5},{22,6},{23,7},{24,8},{25... | collective-permute-start | bytes 393224 | tf_op jit(solution)/shard_map/ppermute | solution.py:19
  8.8 0.9 copy-start
  13.4 4.4 %collective-permute-start.2 = (f32[8,8,3,1,128]{4,1,3,2,0:T(8,128)S(1)}, f32[8,8,3,1,128]{4,1,3,2,0:T(8,128)S(1)}, u32[]{:S(2)}, u32[]{:S(2)}) collective-permute-start(f32[8,8,3,1,128]{4,1,3,2,0:T(8,128)S(1)} %get-tuple-element.286), channel_id=1, source_target_pairs={{4,0},{8,4},{12,8},{5,1},{9,5},{13,9},{6,2},{10,6},{14,10},{7,3},{... | collective-permute-start | bytes 294920 | tf_op jit(solution)/shard_map/ppermute | solution.py:19
  14.7 4.0 %collective-permute-start.3 = (f32[8,8,3,1,128]{4,1,3,2,0:T(8,128)S(1)}, f32[8,8,3,1,128]{4,1,3,2,0:T(8,128)S(1)}, u32[]{:S(2)}, u32[]{:S(2)}) collective-permute-start(f32[8,8,3,1,128]{4,1,3,2,0:T(8,128)S(1)} %get-tuple-element.285), channel_id=1, source_target_pairs={{0,4},{4,8},{8,12},{1,5},{5,9},{9,13},{2,6},{6,10},{10,14},{3,7},{... | collective-permute-start | bytes 294920 | tf_op jit(solution)/shard_map/ppermute | solution.py:16
  19.8 5.7 %collective-permute-start.5 = (f32[8,8,3,6,1]{1,0,4,3,2:T(8,128)S(1)}, f32[8,8,3,6,1]{1,0,4,3,2:T(8,128)S(1)}, u32[]{:S(2)}, u32[]{:S(2)}) collective-permute-start(f32[8,8,3,6,1]{1,0,4,3,2:T(8,128)S(1)} %copy.278), channel_id=1, source_target_pairs={{0,1},{1,2},{2,3},{4,5},{5,6},{6,7},{8,9},{9,10},{10,11},{12,13},{... | collective-permute-start | bytes 13832 | tf_op jit(solution)/shard_map/ppermute | solution.py:16
  24.2 6.5 %collective-permute-start.4 = (f32[8,8,3,6,1]{1,0,4,3,2:T(8,128)S(1)}, f32[8,8,3,6,1]{1,0,4,3,2:T(8,128)S(1)}, u32[]{:S(2)}, u32[]{:S(2)}) collective-permute-start(f32[8,8,3,6,1]{1,0,4,3,2:T(8,128)S(1)} %copy.277), channel_id=1, source_target_pairs={{1,0},{2,1},{3,2},{5,4},{6,5},{7,6},{9,8},{10,9},{11,10},{13,12},{... | collective-permute-start | bytes 13832 | tf_op jit(solution)/shard_map/ppermute | solution.py:19
  83.0 10.6 %collective-permute-start.6 = (f32[8,8,1,4,128]{4,1,3,0,2:T(8,128)S(1)}, f32[8,8,1,4,128]{4,1,3,0,2:T(8,128)S(1)}, u32[]{:S(2)}, u32[]{:S(2)}) collective-permute-start(f32[8,8,1,4,128]{4,1,3,0,2:T(8,128)S(1)} %bitcast.787), channel_id=1, source_target_pairs={{16,0},{17,1},{18,2},{19,3},{20,4},{21,5},{22,6},{23,7},{24,8},{25... | collective-permute-start | bytes 393224 | tf_op jit(solution)/shard_map/ppermute | solution.py:19
  84.3 9.3 %collective-permute-start.7 = (f32[8,8,1,4,128]{4,1,3,0,2:T(8,128)S(1)}, f32[8,8,1,4,128]{4,1,3,0,2:T(8,128)S(1)}, u32[]{:S(2)}, u32[]{:S(2)}) collective-permute-start(f32[8,8,1,4,128]{4,1,3,0,2:T(8,128)S(1)} %bitcast.788), channel_id=1, source_target_pairs={{0,16},{1,17},{2,18},{3,19},{4,20},{5,21},{6,22},{7,23},{8,24},{9,... | collective-permute-start | bytes 393224 | tf_op jit(solution)/shard_map/ppermute | solution.py:16
  90.1 0.7 copy-start.3
  93.7 4.4 %collective-permute-start.8 = (f32[8,8,3,1,128]{4,1,3,0,2:T(8,128)S(1)}, f32[8,8,3,1,128]{4,1,3,0,2:T(8,128)S(1)}, u32[]{:S(2)}, u32[]{:S(2)}) collective-permute-start(f32[8,8,3,1,128]{4,1,3,0,2:T(8,128)S(1)} %get-tuple-element.284), channel_id=1, source_target_pairs={{4,0},{8,4},{12,8},{5,1},{9,5},{13,9},{6,2},{10,6},{14,10},{7,3},{... | collective-permute-start | bytes 294920 | tf_op jit(solution)/shard_map/ppermute | solution.py:19
  95.0 4.0 %collective-permute-start.9 = (f32[8,8,3,1,128]{4,1,3,0,2:T(8,128)S(1)}, f32[8,8,3,1,128]{4,1,3,0,2:T(8,128)S(1)}, u32[]{:S(2)}, u32[]{:S(2)}) collective-permute-start(f32[8,8,3,1,128]{4,1,3,0,2:T(8,128)S(1)} %get-tuple-element.283), channel_id=1, source_target_pairs={{0,4},{4,8},{8,12},{1,5},{5,9},{9,13},{2,6},{6,10},{10,14},{3,7},{... | collective-permute-start | bytes 294920 | tf_op jit(solution)/shard_map/ppermute | solution.py:16
  100.1 4.5 %collective-permute-start.11 = (f32[8,8,3,6,1]{1,0,4,3,2:T(8,128)S(1)}, f32[8,8,3,6,1]{1,0,4,3,2:T(8,128)S(1)}, u32[]{:S(2)}, u32[]{:S(2)}) collective-permute-start(f32[8,8,3,6,1]{1,0,4,3,2:T(8,128)S(1)} %copy.218), channel_id=1, source_target_pairs={{0,1},{1,2},{2,3},{4,5},{5,6},{6,7},{8,9},{9,10},{10,11},{12,13},{... | collective-permute-start | bytes 13832 | tf_op jit(solution)/shard_map/ppermute | solution.py:16
  103.2 6.2 %collective-permute-start.10 = (f32[8,8,3,6,1]{1,0,4,3,2:T(8,128)S(1)}, f32[8,8,3,6,1]{1,0,4,3,2:T(8,128)S(1)}, u32[]{:S(2)}, u32[]{:S(2)}) collective-permute-start(f32[8,8,3,6,1]{1,0,4,3,2:T(8,128)S(1)} %copy.216), channel_id=1, source_target_pairs={{1,0},{2,1},{3,2},{5,4},{6,5},{7,6},{9,8},{10,9},{11,10},{13,12},{... | collective-permute-start | bytes 13832 | tf_op jit(solution)/shard_map/ppermute | solution.py:19
  187.2 7.3 %collective-permute-start.12 = (f32[8,8,1,4,128]{4,1,3,0,2:T(8,128)S(1)}, f32[8,8,1,4,128]{4,1,3,0,2:T(8,128)S(1)}, u32[]{:S(2)}, u32[]{:S(2)}) collective-permute-start(f32[8,8,1,4,128]{4,1,3,0,2:T(8,128)S(1)} %bitcast.804), channel_id=1, source_target_pairs={{16,0},{17,1},{18,2},{19,3},{20,4},{21,5},{22,6},{23,7},{24,8},{25... | collective-permute-start | bytes 393224 | tf_op jit(solution)/shard_map/ppermute | solution.py:19
  188.5 7.1 %collective-permute-start.13 = (f32[8,8,1,4,128]{4,1,3,0,2:T(8,128)S(1)}, f32[8,8,1,4,128]{4,1,3,0,2:T(8,128)S(1)}, u32[]{:S(2)}, u32[]{:S(2)}) collective-permute-start(f32[8,8,1,4,128]{4,1,3,0,2:T(8,128)S(1)} %bitcast.805), channel_id=1, source_target_pairs={{0,16},{1,17},{2,18},{3,19},{4,20},{5,21},{6,22},{7,23},{8,24},{9,... | collective-permute-start | bytes 393224 | tf_op jit(solution)/shard_map/ppermute | solution.py:16
  195.6 4.4 %collective-permute-start.14 = (f32[8,8,3,1,128]{4,1,3,0,2:T(8,128)S(1)}, f32[8,8,3,1,128]{4,1,3,0,2:T(8,128)S(1)}, u32[]{:S(2)}, u32[]{:S(2)}) collective-permute-start(f32[8,8,3,1,128]{4,1,3,0,2:T(8,128)S(1)} %get-tuple-element.282), channel_id=1, source_target_pairs={{4,0},{8,4},{12,8},{5,1},{9,5},{13,9},{6,2},{10,6},{14,10},{7,3},{... | collective-permute-start | bytes 294920 | tf_op jit(solution)/shard_map/ppermute | solution.py:19
  196.9 4.0 %collective-permute-start.15 = (f32[8,8,3,1,128]{4,1,3,0,2:T(8,128)S(1)}, f32[8,8,3,1,128]{4,1,3,0,2:T(8,128)S(1)}, u32[]{:S(2)}, u32[]{:S(2)}) collective-permute-start(f32[8,8,3,1,128]{4,1,3,0,2:T(8,128)S(1)} %get-tuple-element.281), channel_id=1, source_target_pairs={{0,4},{4,8},{8,12},{1,5},{5,9},{9,13},{2,6},{6,10},{10,14},{3,7},{... | collective-permute-start | bytes 294920 | tf_op jit(solution)/shard_map/ppermute | solution.py:16
  200.0 0.9 copy-start.2
  202.0 4.7 %collective-permute-start.17 = (f32[8,8,3,6,1]{1,0,4,3,2:T(8,128)S(1)}, f32[8,8,3,6,1]{1,0,4,3,2:T(8,128)S(1)}, u32[]{:S(2)}, u32[]{:S(2)}) collective-permute-start(f32[8,8,3,6,1]{1,0,4,3,2:T(8,128)S(1)} %copy.230), channel_id=1, source_target_pairs={{0,1},{1,2},{2,3},{4,5},{5,6},{6,7},{8,9},{9,10},{10,11},{12,13},{... | collective-permute-start | bytes 13832 | tf_op jit(solution)/shard_map/ppermute | solution.py:16
  205.3 6.5 %collective-permute-start.16 = (f32[8,8,3,6,1]{1,0,4,3,2:T(8,128)S(1)}, f32[8,8,3,6,1]{1,0,4,3,2:T(8,128)S(1)}, u32[]{:S(2)}, u32[]{:S(2)}) collective-permute-start(f32[8,8,3,6,1]{1,0,4,3,2:T(8,128)S(1)} %copy.228), channel_id=1, source_target_pairs={{1,0},{2,1},{3,2},{5,4},{6,5},{7,6},{9,8},{10,9},{11,10},{13,12},{... | collective-permute-start | bytes 13832 | tf_op jit(solution)/shard_map/ppermute | solution.py:19
